TPU v7x, 64 devices: a 2x2x8 block of a 4x4x8 slice. The times are simulated.
64 devices in a mesh: data: 4 (over x, y), seq: 16 (over z, core).
Axes of the slice: x: 2, y: 2, z: 8, core: 2. Of those that a mesh axis runs over, the one named last changes fastest.
The devices are a block of a 4x4x8 slice.
Arguments:
- x_in: bfloat16 [16, 4096, 2048], P(None, ('data', 'seq')), parts along dimension 1
- positions: int32 [4096], P(('data', 'seq')), parts along dimension 0
- w_query: bfloat16 [3, 2048, 16, 128], replicated
- w_key: bfloat16 [3, 2048, 16, 128], replicated
- w_value: bfloat16 [3, 2048, 16, 128], replicated
- w_out: bfloat16 [3, 16, 128, 2048], replicated
- w_up: bfloat16 [3, 2048, 8192], replicated
- w_down: bfloat16 [3, 8192, 2048], replicated
- g_attn: float32 [3, 2048], replicated
- g_mlp: float32 [3, 2048], replicated
Outputs:
- output: bfloat16 [16, 4096, 2048], P(None, ('data', 'seq')), parts along dimension 1
There are 4 independent parts. A program takes and returns all parts, laid end to end along the dimension named above; an argument that names none is the same for every part.
All inputs are finite; a program needn't handle non-finite values.
Results may differ from a plain program's by a relative error of at most 0.0163719.
Values are sent between devices in bfloat16 or wider.
A program may use at most 768 MiB of HBM per device.

v0:
```python
import jax
import jax.numpy as jnp
from jax import lax
from jax.sharding import PartitionSpec as P

ROPE_BASE = 10000.0
NORM_EPS = 1e-6


def rms_norm(x_act, gain_vec):
    x_f32 = x_act.astype(jnp.float32)
    mean_sq = jnp.mean(x_f32 * x_f32, axis=-1, keepdims=True)
    return (x_f32 * lax.rsqrt(mean_sq + NORM_EPS) * gain_vec).astype(jnp.bfloat16)


def rope_tables(positions, head_dim):
    inv_freq = ROPE_BASE ** (-jnp.arange(head_dim // 2, dtype=jnp.float32) * (2.0 / head_dim))
    angles = positions.astype(jnp.float32)[..., None] * inv_freq
    return jnp.cos(angles), jnp.sin(angles)


def apply_rope(proj_f32, cos_t, sin_t):
    half_dim = proj_f32.shape[-1] // 2
    x_first = proj_f32[..., :half_dim]
    x_second = proj_f32[..., half_dim:]
    cos_b = cos_t[..., None, :]
    sin_b = sin_t[..., None, :]
    return jnp.concatenate([x_first * cos_b - x_second * sin_b, x_second * cos_b + x_first * sin_b], axis=-1).astype(jnp.bfloat16)


def causal_attention(q_heads, k_heads, v_heads, q_offset, q_block):
    n_batch, q_len, kv_heads, groups, head_dim = q_heads.shape
    key_len = k_heads.shape[1]
    n_blocks = q_len // q_block
    att_scale = head_dim ** -0.5
    key_pos = jnp.arange(key_len)

    def one_block(blk_idx):
        blk_start = blk_idx * q_block
        q_blk = lax.dynamic_slice_in_dim(q_heads, blk_start, q_block, axis=1)
        scores = jnp.einsum("bqkgd,bskd->bkgqs", q_blk, k_heads, preferred_element_type=jnp.float32) * att_scale
        query_pos = q_offset + blk_start + jnp.arange(q_block)
        scores = jnp.where(key_pos[None, :] <= query_pos[:, None], scores, -1e30)
        row_max = jnp.max(scores, axis=-1, keepdims=True)
        exp_f32 = jnp.exp(scores - row_max)
        row_sum = jnp.sum(exp_f32, axis=-1)
        weighted = jnp.einsum("bkgqs,bskd->bqkgd", exp_f32.astype(jnp.bfloat16), v_heads, preferred_element_type=jnp.float32)
        return (weighted / jnp.transpose(row_sum, (0, 3, 1, 2))[..., None]).astype(jnp.bfloat16)

    blocks = lax.map(one_block, jnp.arange(n_blocks))
    return jnp.moveaxis(blocks, 0, 1).reshape(n_batch, q_len, kv_heads * groups, head_dim)


def layer_step(hidden, cos_t, sin_t, w_query, w_key, w_value, w_out, w_up, w_down, gain_attn, gain_mlp):
    normed = rms_norm(hidden, gain_attn)
    q_loc = apply_rope(jnp.einsum("bsd,dhe->bshe", normed, w_query, preferred_element_type=jnp.float32), cos_t, sin_t)
    k_loc = apply_rope(jnp.einsum("bsd,dhe->bshe", normed, w_key, preferred_element_type=jnp.float32), cos_t, sin_t)
    v_loc = jnp.einsum("bsd,dhe->bshe", normed, w_value, preferred_element_type=jnp.float32).astype(jnp.bfloat16)
    q_all = lax.all_to_all(q_loc, "seq", 2, 1, tiled=True)
    k_all = lax.all_to_all(k_loc, "seq", 2, 1, tiled=True)
    v_all = lax.all_to_all(v_loc, "seq", 2, 1, tiled=True)
    n_batch, seq_len, heads_loc, head_dim = q_all.shape
    kv_loc = k_all.shape[2]
    q_grouped = q_all.reshape(n_batch, seq_len, kv_loc, heads_loc // kv_loc, head_dim)
    attn_heads = causal_attention(q_grouped, k_all, v_all, 0, min(256, seq_len))
    attn_loc = lax.all_to_all(attn_heads, "seq", 1, 2, tiled=True)
    resid_h = (hidden.astype(jnp.float32) + jnp.einsum("bshe,hed->bsd", attn_loc, w_out, preferred_element_type=jnp.float32)).astype(jnp.bfloat16)
    normed_mlp = rms_norm(resid_h, gain_mlp)
    gelu_act = jax.nn.gelu(jnp.einsum("bsd,df->bsf", normed_mlp, w_up, preferred_element_type=jnp.float32), approximate=True).astype(jnp.bfloat16)
    layer_out = resid_h.astype(jnp.float32) + jnp.einsum("bsf,fd->bsd", gelu_act, w_down, preferred_element_type=jnp.float32)
    return layer_out.astype(jnp.bfloat16)


def solution(mesh):
    tok_spec = P(None, ("data", "seq"), None)
    in_specs = (tok_spec, P(("data", "seq"))) + (P(),) * 8

    def device_fn(x_loc, pos_loc, w_query, w_key, w_value, w_out, w_up, w_down, g_attn, g_mlp):
        cos_t, sin_t = rope_tables(pos_loc, w_query.shape[-1])
        hidden = x_loc
        for layer_idx in range(w_query.shape[0]):
            hidden = layer_step(hidden, cos_t, sin_t, w_query[layer_idx], w_key[layer_idx], w_value[layer_idx], w_out[layer_idx], w_up[layer_idx], w_down[layer_idx], g_attn[layer_idx], g_mlp[layer_idx])
        return hidden

    return jax.shard_map(device_fn, mesh=mesh, in_specs=in_specs, out_specs=tok_spec, check_vma=False)
```

profile of v0, /device:TPU:21, one launch (start us, length us, event | category | flops | bytes accessed | tf_op | source)
XLA Modules:
  0.0 1919.1 jit_solution(10069000410647459593)
XLA Ops:
  61.1 19.6 %subtract_convert_fusion.4 = (bf16[16,64,16,64]{3,1,2,0:T(8,128)(2,1)}, bf16[16,64,16,64]{3,1,2,0:T(8,128)(2,1)}, bf16[16,64,16,64]{3,1,2,0:T(8,128)(2,1)}, bf16[16,64,16,64]{3,1,2,0:T(8,128)(2,1)}) fusion(f32[16,64,16,128]{3,1,2,0:T(8,128)} %fusion.202, f32[64,64]{1,0:T(8,128)S(1)} %get-tuple-element.237, f32[64,64]{1,0:T(8,128)S(1)} %get-tuple-element.236, ...), kind=kLoop, calls=%fused_computation.210 | loop fusion | flops 16777216 | bytes 25198592 | tf_op jit(solution)/shard_map/convert.8
  106.8 85.2 %all-to-all-done.1 = bf16[16,64,16,128]{3,1,0,2:T(8,128)(2,1)} async-done(((bf16[16,64,16,128]{3,1,0,2:T(8,128)(2,1)}), bf16[16,64,16,128]{3,1,0,2:T(8,128)(2,1)}, u32[]{:S(2)}, u32[]{:S(2)}) %all-to-all-start.1) | async-done | bytes 4194336 | tf_op jit(solution)/shard_map/all_to_all | solution.py:60
  228.4 65.3 %all-to-all-done = bf16[16,64,16,128]{3,1,0,2:T(8,128)(2,1)} async-done(((bf16[16,64,16,128]{3,1,0,2:T(8,128)(2,1)}), bf16[16,64,16,128]{3,1,0,2:T(8,128)(2,1)}, u32[]{:S(2)}, u32[]{:S(2)}) %all-to-all-start) | async-done | bytes 4194336 | tf_op jit(solution)/shard_map/all_to_all | solution.py:59
  314.4 81.3 %all-to-all-done.2 = bf16[16,64,16,128]{3,1,0,2:T(8,128)(2,1)} async-done(((bf16[16,64,16,128]{3,1,0,2:T(8,128)(2,1)}), bf16[16,64,16,128]{3,1,0,2:T(8,128)(2,1)}, u32[]{:S(2)}, u32[]{:S(2)}) %all-to-all-start.2) | async-done | bytes 4194336 | tf_op jit(solution)/shard_map/all_to_all | solution.py:61
  404.3 70.4 %while.33 = (s32[]{:T(128)}, bf16[4,16,256,1,1,128]{5,2,0,1,4,3:T(8,128)(2,1)}, s32[4]{0:T(128)S(1)}, bf16[16,1024,1,1,128]{4,1,0,3,2:T(8,128)(2,1)}, bf16[16,10...) while((s32[]{:T(128)}, ...), condition=%wide.region_4.5_spmd.clone, body=%wide.region_1.4_spmd.clone.sunk | while | flops 2194923776 | bytes 78727872 | solution.py:50
  491.9 91.8 %all-to-all-done.3 = bf16[16,1024,1,128]{3,0,2,1:T(8,128)(2,1)} async-done(((bf16[16,1024,1,128]{3,0,2,1:T(8,128)(2,1)}), bf16[16,1024,1,128]{3,0,2,1:T(8,128)(2,1)}, u32[]{:S(2)}, u32[]{:S(2)}) %all-to-all-start.3) | async-done | bytes 4194336 | tf_op jit(solution)/shard_map/all_to_all | solution.py:66
  599.4 47.0 %fusion.244.clone.5 = bf16[16,64,8192]{2,1,0:T(8,128)(2,1)} fusion(bf16[3,2048,8192]{2,1,0:T(8,128)(2,1)} %param.22, bf16[16,64,2048]{2,1,0:T(8,128)(2,1)} %get-tuple-element.239, f32[2048]{0:T(1024)S(1)} %bitcast.543, f32[16,64]{1,0:T(8,128)S(1)} %add_rsqrt_fusion.4), kind=kOutput, calls=%fused_computation.88.clone.clone.clone.clone.clone.clone.2 | convolution fusion | flops 34443624448 | bytes 54538240 | tf_op jit(solution)/shard_map/bsd,df->bsf/dot_general | solution.py:69
  646.4 45.6 %fusion.179 = (f32[16,64]{1,0:T(8,128)S(1)}, bf16[16,64,2048]{2,1,0:T(8,128)(2,1)}) fusion(bf16[3,8192,2048]{2,1,0:T(8,128)(2,1)} %param.23, bf16[16,64,2048]{2,1,0:T(8,128)(2,1)} %get-tuple-element.239, bf16[16,64,8192]{2,1,0:T(8,128)(2,1)} %fusion.244.clone.5), kind=kOutput, calls=%fused_computation.158 | convolution fusion | flops 34372321280 | bytes 58724352 | tf_op jit(solution)/shard_map/bsf,fd->bsd/dot_general | solution.py:70
  745.7 19.3 %subtract_convert_fusion.2 = (bf16[16,64,16,64]{3,1,2,0:T(8,128)(2,1)}, bf16[16,64,16,64]{3,1,2,0:T(8,128)(2,1)}, bf16[16,64,16,64]{3,1,2,0:T(8,128)(2,1)}, bf16[16,64,16,64]{3,1,2,0:T(8,128)(2,1)}) fusion(f32[16,64,16,128]{3,1,2,0:T(8,128)} %fusion.199, f32[64,64]{1,0:T(8,128)S(1)} %copy-done.11, f32[64,64]{1,0:T(8,128)S(1)} %copy-done.8, ...), kind=kLoop, calls=%fused_computation.205 | loop fusion | flops 16777216 | bytes 25198592 | tf_op jit(solution)/shard_map/convert.4
  772.6 37.5 %all-to-all-done.6 = bf16[16,64,16,128]{3,1,0,2:T(8,128)(2,1)} async-done(((bf16[16,64,16,128]{3,1,0,2:T(8,128)(2,1)}), bf16[16,64,16,128]{3,1,0,2:T(8,128)(2,1)}, u32[]{:S(2)}, u32[]{:S(2)}) %all-to-all-start.6) | async-done | bytes 4194336 | tf_op jit(solution)/shard_map/all_to_all | solution.py:61
  827.2 85.2 %all-to-all-done.5 = bf16[16,64,16,128]{3,1,0,2:T(8,128)(2,1)} async-done(((bf16[16,64,16,128]{3,1,0,2:T(8,128)(2,1)}), bf16[16,64,16,128]{3,1,0,2:T(8,128)(2,1)}, u32[]{:S(2)}, u32[]{:S(2)}) %all-to-all-start.5) | async-done | bytes 4194336 | tf_op jit(solution)/shard_map/all_to_all | solution.py:60
  932.5 81.7 %all-to-all-done.4 = bf16[16,64,16,128]{3,1,0,2:T(8,128)(2,1)} async-done(((bf16[16,64,16,128]{3,1,0,2:T(8,128)(2,1)}), bf16[16,64,16,128]{3,1,0,2:T(8,128)(2,1)}, u32[]{:S(2)}, u32[]{:S(2)}) %all-to-all-start.4) | async-done | bytes 4194336 | tf_op jit(solution)/shard_map/all_to_all | solution.py:59
  1022.8 69.9 %while.34 = (s32[]{:T(128)}, bf16[4,16,256,1,1,128]{5,2,0,1,4,3:T(8,128)(2,1)}, s32[4]{0:T(128)S(1)}, bf16[16,1024,1,1,128]{4,1,0,3,2:T(8,128)(2,1)}, bf16[16,10...) while((s32[]{:T(128)}, ...), condition=%wide.region_10.11_spmd.clone, body=%wide.region_7.10_spmd.clone.sunk | while | flops 2194923776 | bytes 78727872 | solution.py:50
  1097.6 104.9 %all_to_all.207 = bf16[16,1024,1,128]{3,0,2,1:T(8,128)(2,1)S(1)} all-to-all(bf16[16,1024,1,128]{3,0,2,1:T(8,128)(2,1)S(1)} %copy.81), channel_id=1, replica_groups=mesh['data'=4,'seq'=16] {'seq'}, dimensions={1} | all-to-all | bytes 8388608 | tf_op jit(solution)/shard_map/all_to_all | solution.py:66
  1217.1 46.0 %fusion.233.clone.5 = bf16[16,64,8192]{2,1,0:T(8,128)(2,1)} fusion(bf16[3,2048,8192]{2,1,0:T(8,128)(2,1)} %param.22, bf16[16,64,2048]{2,1,0:T(8,128)(2,1)S(1)} %get-tuple-element.243, f32[2048]{0:T(1024)S(1)} %bitcast.539, f32[16,64]{1,0:T(8,128)S(1)} %add_rsqrt_fusion.2), kind=kOutput, calls=%fused_computation.96.clone.clone.clone.clone.clone.clone.2 | convolution fusion | flops 34443624448 | bytes 54538240 | tf_op jit(solution)/shard_map/bsd,df->bsf/dot_general | solution.py:69
  1263.0 45.4 %fusion.187 = (f32[16,64]{1,0:T(8,128)S(1)}, bf16[16,64,2048]{2,1,0:T(8,128)(2,1)}) fusion(bf16[3,8192,2048]{2,1,0:T(8,128)(2,1)} %param.23, bf16[16,64,2048]{2,1,0:T(8,128)(2,1)} %copy-done.23, bf16[16,64,8192]{2,1,0:T(8,128)(2,1)} %fusion.233.clone.5), kind=kOutput, calls=%fused_computation.166 | convolution fusion | flops 34372321280 | bytes 58724352 | tf_op jit(solution)/shard_map/bsf,fd->bsd/dot_general | solution.py:70
  1357.6 19.4 %subtract_convert_fusion = (bf16[16,64,16,64]{3,1,2,0:T(8,128)(2,1)}, bf16[16,64,16,64]{3,1,2,0:T(8,128)(2,1)}, bf16[16,64,16,64]{3,1,2,0:T(8,128)(2,1)}, bf16[16,64,16,64]{3,1,2,0:T(8,128)(2,1)}) fusion(f32[16,64,16,128]{3,1,2,0:T(8,128)} %fusion.196, f32[64,64]{1,0:T(8,128)S(1)} %copy-done.12, f32[64,64]{1,0:T(8,128)S(1)} %copy-done.9, ...), kind=kLoop, calls=%fused_computation.200 | loop fusion | flops 16777216 | bytes 25198592 | tf_op jit(solution)/shard_map/convert
  1384.5 37.6 %all-to-all-done.10 = bf16[16,64,16,128]{3,1,0,2:T(8,128)(2,1)} async-done(((bf16[16,64,16,128]{3,1,0,2:T(8,128)(2,1)}), bf16[16,64,16,128]{3,1,0,2:T(8,128)(2,1)}, u32[]{:S(2)}, u32[]{:S(2)}) %all-to-all-start.10) | async-done | bytes 4194336 | tf_op jit(solution)/shard_map/all_to_all | solution.py:61
  1437.8 85.2 %all-to-all-done.9 = bf16[16,64,16,128]{3,1,0,2:T(8,128)(2,1)} async-done(((bf16[16,64,16,128]{3,1,0,2:T(8,128)(2,1)}), bf16[16,64,16,128]{3,1,0,2:T(8,128)(2,1)}, u32[]{:S(2)}, u32[]{:S(2)}) %all-to-all-start.9) | async-done | bytes 4194336 | tf_op jit(solution)/shard_map/all_to_all | solution.py:60
  1543.1 81.7 %all-to-all-done.8 = bf16[16,64,16,128]{3,1,0,2:T(8,128)(2,1)} async-done(((bf16[16,64,16,128]{3,1,0,2:T(8,128)(2,1)}), bf16[16,64,16,128]{3,1,0,2:T(8,128)(2,1)}, u32[]{:S(2)}, u32[]{:S(2)}) %all-to-all-start.8) | async-done | bytes 4194336 | tf_op jit(solution)/shard_map/all_to_all | solution.py:59
  1633.4 69.9 %while.35 = (s32[]{:T(128)}, bf16[4,16,256,1,1,128]{5,2,0,1,4,3:T(8,128)(2,1)}, s32[4]{0:T(128)S(1)}, bf16[16,1024,1,1,128]{4,1,0,3,2:T(8,128)(2,1)}, bf16[16,10...) while((s32[]{:T(128)}, ...), condition=%wide.region_16.17_spmd.clone, body=%wide.region_13.16_spmd.clone.sunk | while | flops 2194923776 | bytes 78727872 | solution.py:50
  1708.2 105.0 %all_to_all.208 = bf16[16,1024,1,128]{3,0,2,1:T(8,128)(2,1)S(1)} all-to-all(bf16[16,1024,1,128]{3,0,2,1:T(8,128)(2,1)S(1)} %copy.93), channel_id=1, replica_groups=mesh['data'=4,'seq'=16] {'seq'}, dimensions={1} | all-to-all | bytes 8388608 | tf_op jit(solution)/shard_map/all_to_all | solution.py:66
  1827.7 46.0 %fusion.336 = bf16[16,64,8192]{2,1,0:T(8,128)(2,1)} fusion(bf16[3,2048,8192]{2,1,0:T(8,128)(2,1)} %param.22, bf16[16,64,2048]{2,1,0:T(8,128)(2,1)S(1)} %get-tuple-element.247, f32[2048]{0:T(1024)S(1)} %bitcast.535, f32[16,64]{1,0:T(8,128)S(1)} %add_rsqrt_fusion), kind=kOutput, calls=%fused_computation.104.clone.clone.clone.clone.2 | convolution fusion | flops 34443624448 | bytes 54538240 | tf_op jit(solution)/shard_map/bsd,df->bsf/dot_general | solution.py:69
  1873.7 44.9 %fusion.194 = bf16[16,64,2048]{2,1,0:T(8,128)(2,1)} fusion(bf16[16,64,2048]{2,1,0:T(8,128)(2,1)} %copy-done.24, bf16[3,8192,2048]{2,1,0:T(8,128)(2,1)} %param.23, bf16[16,64,8192]{2,1,0:T(8,128)(2,1)} %fusion.336), kind=kOutput, calls=%fused_computation.173 | convolution fusion | flops 34366029824 | bytes 58720256 | tf_op jit(solution)/shard_map/bsf,fd->bsd/dot_general | solution.py:70
  (226 shorter events, 635.3 us)
Async XLA Ops:
  0.0 23.7 %slice-start = ((s8[25165824]{0:T(1024)(128)(4,1)}), s8[4194304]{0:T(1024)(128)(4,1)S(1)}, s32[]{:S(2)}) async-start(s8[25165824]{0:T(1024)(128)(4,1)} %bitcast.521), calls=%async_computation.12 | async-start | bytes 8388608
  1.6 22.2 %slice-start.1 = ((s8[25165824]{0:T(1024)(128)(4,1)}), s8[4194304]{0:T(1024)(128)(4,1)S(1)}, s32[]{:S(2)}) async-start(s8[25165824]{0:T(1024)(128)(4,1)} %bitcast.521), calls=%async_computation.13 | async-start | bytes 8388608
  1.6 22.2 %slice-start.2 = ((s8[25165824]{0:T(1024)(128)(4,1)}), s8[4194304]{0:T(1024)(128)(4,1)S(1)}, s32[]{:S(2)}) async-start(s8[25165824]{0:T(1024)(128)(4,1)} %bitcast.521), calls=%async_computation.14 | async-start | bytes 8388608
  1.6 22.2 %slice-start.3 = ((s8[25165824]{0:T(1024)(128)(4,1)}), s8[4194304]{0:T(1024)(128)(4,1)S(1)}, s32[]{:S(2)}) async-start(s8[25165824]{0:T(1024)(128)(4,1)} %bitcast.521), calls=%async_computation.15 | async-start | bytes 8388608
  1.6 23.2 %slice-start.4 = ((s8[25165824]{0:T(1024)(128)(4,1)}), s8[4194304]{0:T(1024)(128)(4,1)S(1)}, s32[]{:S(2)}) async-start(s8[25165824]{0:T(1024)(128)(4,1)} %bitcast.521), calls=%async_computation.16 | async-start | bytes 8388608
  1.6 24.3 %slice-start.5 = ((s8[25165824]{0:T(1024)(128)(4,1)}), s8[4194304]{0:T(1024)(128)(4,1)S(1)}, s32[]{:S(2)}) async-start(s8[25165824]{0:T(1024)(128)(4,1)} %bitcast.521), calls=%async_computation.17 | async-start | bytes 8388608
  61.1 19.7 %copy-start.7 = (f32[64,64]{1,0:T(8,128)}, f32[64,64]{1,0:T(8,128)S(1)}, u32[]{:S(2)}) copy-start(f32[64,64]{1,0:T(8,128)S(1)} %get-tuple-element.236) | copy-start | bytes 49156
  61.1 19.7 %copy-start.10 = (f32[64,64]{1,0:T(8,128)}, f32[64,64]{1,0:T(8,128)S(1)}, u32[]{:S(2)}) copy-start(f32[64,64]{1,0:T(8,128)S(1)} %get-tuple-element.237) | copy-start | bytes 49156
  88.4 103.5 %all-to-all-start.1 = ((bf16[16,64,16,128]{3,1,0,2:T(8,128)(2,1)}), bf16[16,64,16,128]{3,1,0,2:T(8,128)(2,1)}, u32[]{:S(2)}, u32[]{:S(2)}) async-start(bf16[16,64,16,128]{3,1,0,2:T(8,128)(2,1)} %copy.63), calls=%async_computation.1 | async-start | bytes 8388608 | tf_op jit(solution)/shard_map/all_to_all | solution.py:60
  191.9 101.8 %all-to-all-start = ((bf16[16,64,16,128]{3,1,0,2:T(8,128)(2,1)}), bf16[16,64,16,128]{3,1,0,2:T(8,128)(2,1)}, u32[]{:S(2)}, u32[]{:S(2)}) async-start(bf16[16,64,16,128]{3,1,0,2:T(8,128)(2,1)} %copy.60), calls=%async_computation | async-start | bytes 8388608 | tf_op jit(solution)/shard_map/all_to_all | solution.py:59
  200.9 14.8 copy-start.2
  293.7 102.0 %all-to-all-start.2 = ((bf16[16,64,16,128]{3,1,0,2:T(8,128)(2,1)}), bf16[16,64,16,128]{3,1,0,2:T(8,128)(2,1)}, u32[]{:S(2)}, u32[]{:S(2)}) async-start(bf16[16,64,16,128]{3,1,0,2:T(8,128)(2,1)} %copy.66), calls=%async_computation.2 | async-start | bytes 8388608 | tf_op jit(solution)/shard_map/all_to_all | solution.py:61
  474.7 16.6 copy-start.13
  481.6 102.1 %all-to-all-start.3 = ((bf16[16,1024,1,128]{3,0,2,1:T(8,128)(2,1)}), bf16[16,1024,1,128]{3,0,2,1:T(8,128)(2,1)}, u32[]{:S(2)}, u32[]{:S(2)}) async-start(bf16[16,1024,1,128]{3,0,2,1:T(8,128)(2,1)} %copy.69), calls=%async_computation.3 | async-start | bytes 8388608 | tf_op jit(solution)/shard_map/all_to_all | solution.py:66
  646.4 45.6 %copy-start.16 = (f32[1,2048]{1,0:T(1,128)S(1)}, f32[1,2048]{1,0:T(1,128)}, u32[]{:S(2)}) copy-start(f32[1,2048]{1,0:T(1,128)} %get-tuple-element.235) | copy-start | bytes 24580
  708.0 102.1 %all-to-all-start.6 = ((bf16[16,64,16,128]{3,1,0,2:T(8,128)(2,1)}), bf16[16,64,16,128]{3,1,0,2:T(8,128)(2,1)}, u32[]{:S(2)}, u32[]{:S(2)}) async-start(bf16[16,64,16,128]{3,1,0,2:T(8,128)(2,1)} %copy.78), calls=%async_computation.6 | async-start | bytes 8388608 | tf_op jit(solution)/shard_map/all_to_all | solution.py:61
  810.1 102.3 %all-to-all-start.5 = ((bf16[16,64,16,128]{3,1,0,2:T(8,128)(2,1)}), bf16[16,64,16,128]{3,1,0,2:T(8,128)(2,1)}, u32[]{:S(2)}, u32[]{:S(2)}) async-start(bf16[16,64,16,128]{3,1,0,2:T(8,128)(2,1)} %copy.75), calls=%async_computation.5 | async-start | bytes 8388608 | tf_op jit(solution)/shard_map/all_to_all | solution.py:60
  912.3 101.8 %all-to-all-start.4 = ((bf16[16,64,16,128]{3,1,0,2:T(8,128)(2,1)}), bf16[16,64,16,128]{3,1,0,2:T(8,128)(2,1)}, u32[]{:S(2)}, u32[]{:S(2)}) async-start(bf16[16,64,16,128]{3,1,0,2:T(8,128)(2,1)} %copy.72), calls=%async_computation.4 | async-start | bytes 8388608 | tf_op jit(solution)/shard_map/all_to_all | solution.py:59
  1097.6 106.0 %copy-start.22 = (bf16[16,64,2048]{2,1,0:T(8,128)(2,1)S(1)}, bf16[16,64,2048]{2,1,0:T(8,128)(2,1)}, u32[]{:S(2)}) copy-start(bf16[16,64,2048]{2,1,0:T(8,128)(2,1)} %get-tuple-element.241) | copy-start | bytes 12582916
  1263.0 45.4 %copy-start.14 = (f32[1,2048]{1,0:T(1,128)S(1)}, f32[1,2048]{1,0:T(1,128)}, u32[]{:S(2)}) copy-start(f32[1,2048]{1,0:T(1,128)} %get-tuple-element.233) | copy-start | bytes 24580
  1324.4 97.7 %all-to-all-start.10 = ((bf16[16,64,16,128]{3,1,0,2:T(8,128)(2,1)}), bf16[16,64,16,128]{3,1,0,2:T(8,128)(2,1)}, u32[]{:S(2)}, u32[]{:S(2)}) async-start(bf16[16,64,16,128]{3,1,0,2:T(8,128)(2,1)} %copy.90), calls=%async_computation.10 | async-start | bytes 8388608 | tf_op jit(solution)/shard_map/all_to_all | solution.py:61
  1422.1 100.8 %all-to-all-start.9 = ((bf16[16,64,16,128]{3,1,0,2:T(8,128)(2,1)}), bf16[16,64,16,128]{3,1,0,2:T(8,128)(2,1)}, u32[]{:S(2)}, u32[]{:S(2)}) async-start(bf16[16,64,16,128]{3,1,0,2:T(8,128)(2,1)} %copy.87), calls=%async_computation.9 | async-start | bytes 8388608 | tf_op jit(solution)/shard_map/all_to_all | solution.py:60
  1523.0 101.8 %all-to-all-start.8 = ((bf16[16,64,16,128]{3,1,0,2:T(8,128)(2,1)}), bf16[16,64,16,128]{3,1,0,2:T(8,128)(2,1)}, u32[]{:S(2)}, u32[]{:S(2)}) async-start(bf16[16,64,16,128]{3,1,0,2:T(8,128)(2,1)} %copy.84), calls=%async_computation.8 | async-start | bytes 8388608 | tf_op jit(solution)/shard_map/all_to_all | solution.py:59
  1708.2 106.1 %copy-start.20 = (bf16[16,64,2048]{2,1,0:T(8,128)(2,1)S(1)}, bf16[16,64,2048]{2,1,0:T(8,128)(2,1)}, u32[]{:S(2)}) copy-start(bf16[16,64,2048]{2,1,0:T(8,128)(2,1)} %get-tuple-element.245) | copy-start | bytes 12582916
  (26 other events, 212.2 us)
where the time goes:
time: 1930 us; the launch traced here: 1920 us
  waiting for transfers between devices  732 us (38%)
  matrix products  566 us (29%)
  blocking collectives  210 us (11%)
  local copies, waits for them, and re-layouts  166 us (9%)
  other arithmetic  147 us (8%)
  starting transfers between devices  89.3 us (5%)
    all_to_all x3, waiting for transfers between devices, layer_step(): k_all = lax.all_to_all(k_loc, 'seq', 2, 1, tiled=True)  255 us
    all_to_all x3, waiting for transfers between devices, layer_step(): q_all = lax.all_to_all(q_loc, 'seq', 2, 1, tiled=True)  229 us
    all_to_all x2, blocking collectives, layer_step(): attn_loc = lax.all_to_all(attn_heads, 'seq', 1, 2, tiled=True)  210 us
    all_to_all x3, waiting for transfers between devices, layer_step(): v_all = lax.all_to_all(v_loc, 'seq', 2, 1, tiled=True)  156 us
    dot_general x3, matrix products, layer_step(): jnp.einsum('bsd,df->bsf', normed_mlp, w_up, preferred_element_type=jnp.fl...  139 us
    dot_general x3, matrix products, layer_step(): jnp.einsum('bsf,fd->bsd', gelu_act, w_down, preferred_element_type=jnp.fl...  136 us
    all_to_all x1, waiting for transfers between devices, layer_step(): attn_loc = lax.all_to_all(attn_heads, 'seq', 1, 2, tiled=True)  91.8 us
    dot_general x12, matrix products, one_block(): jnp.einsum('bkgqs,bskd->bqkgd', exp_f32.astype(jnp.bfloat16), v_heads, pr...  79 us
  transfers between devices with their start and end apart: 10, of which 10 were waited for; matrix products, arithmetic and copies ran while one was open for 10% of the time, Pallas kernels for 0%

commit v1 on v0

v1 whole, which is shorter than its diff:
```python
import functools
import jax
import jax.numpy as jnp
from jax import lax
from jax.experimental import pallas as pl
from jax.experimental.pallas import tpu as pltpu
from jax.sharding import PartitionSpec as P

EPS = 1e-6
F32 = jnp.float32
BF16 = jnp.bfloat16


def norm_rows(x, g):
    x = x.astype(F32)
    return (x * lax.rsqrt(jnp.mean(x * x, axis=-1, keepdims=True) + EPS) * g).astype(BF16)


def gelu(x):
    h = 0.5 * x
    return h * jnp.tanh(x * (0.7978845608028654 + 0.035677408136300125 * (x * x))) + h


def row_loop(rows, tile, body):
    if rows == tile:
        body(0)
        return
    def step(i, c):
        body(pl.multiple_of(i * tile, tile))
        return c
    lax.fori_loop(0, rows // tile, step, 0)


def qkv_kernel(nq, tm, x_ref, g_ref, cos_ref, sin_ref, wq, wk, wv, q_ref, k_ref, v_ref, n_ref):
    s = pl.program_id(0)
    rows = x_ref.shape[0]
    dh = cos_ref.shape[1]

    @pl.when(s == 0)
    def _():
        def nb(r):
            n_ref[pl.ds(r, 128), :] = norm_rows(x_ref[pl.ds(r, 128), :], g_ref[0])
        row_loop(rows, 128, nb)

    def proj(w_ref, o_ref, rope):
        def mb(r):
            u = jnp.dot(n_ref[pl.ds(r, tm), :], w_ref[0], preferred_element_type=F32)
            if not rope:
                o_ref[pl.ds(r, tm), :] = u.astype(BF16)
            else:
                c = cos_ref[pl.ds(r, tm), :]
                sn = sin_ref[pl.ds(r, tm), :]
                for h in range(u.shape[1] // dh):
                    uh = u[:, h * dh:(h + 1) * dh]
                    o_ref[pl.ds(r, tm), h * dh:(h + 1) * dh] = (uh * c + pltpu.roll(uh, dh // 2, 1) * sn).astype(BF16)
        row_loop(rows, tm, mb)

    pl.when(s < nq)(lambda: proj(wq, q_ref, True))
    pl.when((s >= nq) & (s < 2 * nq))(lambda: proj(wk, k_ref, True))
    pl.when(s >= 2 * nq)(lambda: proj(wv, v_ref, False))


def qkv_call(x, g, cos, sin, wq, wk, wv, layer, tn=512, tm=512):
    rows, d = x.shape
    hd = wq.shape[2]
    nq = hd // tn
    def wmap(i):
        return lambda s: (layer, 0, jnp.clip(s - i * nq, 0, nq - 1))
    def omap(i):
        return lambda s: (0, jnp.clip(s - i * nq, 0, nq - 1))
    full = lambda a: pl.BlockSpec(a.shape, lambda s: (0,) * a.ndim)
    out = jax.ShapeDtypeStruct((rows, hd), BF16)
    return pl.pallas_call(
        functools.partial(qkv_kernel, nq, tm),
        grid=(3 * nq,),
        in_specs=[full(x), pl.BlockSpec((1, 1, d), lambda s: (layer, 0, 0)), full(cos), full(sin)]
        + [pl.BlockSpec((1, d, tn), wmap(i)) for i in range(3)],
        out_specs=[pl.BlockSpec((rows, tn), omap(i)) for i in range(3)],
        out_shape=[out, out, out],
        scratch_shapes=[pltpu.VMEM((rows, d), BF16)],
        compiler_params=pltpu.CompilerParams(vmem_limit_bytes=56 * 2**20),
        cost_estimate=pl.CostEstimate(flops=6 * rows * d * hd, bytes_accessed=6 * d * hd, transcendentals=0),
        name="qkv",
    )(x, g, cos, sin, wq, wk, wv)


def attn_kernel(dh, tq, q_ref, k_ref, v_ref, o_ref):
    rows = q_ref.shape[0]
    scale = dh ** -0.5 * 1.4426950408889634
    r = lax.broadcasted_iota(jnp.int32, (tq, tq), 0)
    c = lax.broadcasted_iota(jnp.int32, (tq, tq), 1)
    keep = c <= r
    jobs = [(h, i) for h in range(q_ref.shape[1] // dh) for i in range(rows // tq)]
    def score(job):
        h, i = job
        cs = slice(h * dh, (h + 1) * dh)
        n = (i + 1) * tq
        return lax.dot_general(q_ref[i * tq:n, cs], k_ref[:n, cs], (((1,), (1,)), ((), ())), preferred_element_type=F32)
    nxt = score(jobs[0])
    for j, (h, i) in enumerate(jobs):
        s = nxt
        if j + 1 < len(jobs):
            nxt = score(jobs[j + 1])
        cs = slice(h * dh, (h + 1) * dh)
        n = (i + 1) * tq
        sd = jnp.where(keep, s[:, n - tq:], -1e30)
        s = jnp.concatenate([s[:, :n - tq], sd], axis=1) if i else sd
        m = jnp.max(s, axis=1, keepdims=True)
        e = jnp.exp2((s - m) * scale)
        l = jnp.sum(e, axis=1, keepdims=True)
        o = jnp.dot(e.astype(BF16), v_ref[:n, cs], preferred_element_type=F32)
        o_ref[i * tq:n, cs] = (o / l).astype(BF16)


def attn_call(q, k, v, dh=128, tq=256, hb=1):
    rows, hd = q.shape
    spec = pl.BlockSpec((rows, dh * hb), lambda h: (0, h))
    return pl.pallas_call(
        functools.partial(attn_kernel, dh, tq),
        grid=(hd // dh // hb,),
        in_specs=[spec] * 3,
        out_specs=spec,
        out_shape=jax.ShapeDtypeStruct((rows, hd), BF16),
        compiler_params=pltpu.CompilerParams(vmem_limit_bytes=56 * 2**20),
        cost_estimate=pl.CostEstimate(flops=2 * rows * rows * hd, bytes_accessed=8 * rows * hd, transcendentals=0),
        name="attn",
    )(q, k, v)


def mlp_kernel(no, nf, tm, o_ref, x_ref, g_ref, wo, wu, wd, y_ref, h_ref, r_ref, acc_ref):
    s = pl.program_id(0)
    rows, d = x_ref.shape
    tn = wo.shape[2]

    @pl.when(s < no)
    def _():
        def mb(r):
            cs = pl.ds(pl.multiple_of(s * tn, tn), tn)
            u = jnp.dot(o_ref[pl.ds(r, tm), :], wo[0], preferred_element_type=F32)
            h_ref[pl.ds(r, tm), cs] = (x_ref[pl.ds(r, tm), cs].astype(F32) + u).astype(BF16)
        row_loop(rows, tm, mb)

    @pl.when(s == no)
    def _():
        def nb(r):
            h = h_ref[pl.ds(r, 128), :]
            r_ref[pl.ds(r, 128), :] = norm_rows(h, g_ref[0])
            acc_ref[pl.ds(r, 128), :] = h.astype(F32)
        row_loop(rows, 128, nb)

    @pl.when(s >= no)
    def _():
        def mb(r):
            z = jnp.dot(r_ref[pl.ds(r, tm), :], wu[0], preferred_element_type=F32)
            z = gelu(z).astype(BF16)
            acc_ref[pl.ds(r, tm), :] += jnp.dot(z, wd[0], preferred_element_type=F32)
        row_loop(rows, tm, mb)

    @pl.when(s == no + nf - 1)
    def _():
        def nb(r):
            y_ref[pl.ds(r, 128), :] = acc_ref[pl.ds(r, 128), :].astype(BF16)
        row_loop(rows, 128, nb)


def mlp_call(o, x, g, wo, wu, wd, layer, tn=512, tf=512, tm=512):
    rows, d = x.shape
    f = wu.shape[2]
    no, nf = d // tn, f // tf
    full = lambda a: pl.BlockSpec(a.shape, lambda s: (0,) * a.ndim)
    return pl.pallas_call(
        functools.partial(mlp_kernel, no, nf, tm),
        grid=(no + nf,),
        in_specs=[full(o), full(x), pl.BlockSpec((1, 1, d), lambda s: (layer, 0, 0)),
                  pl.BlockSpec((1, wo.shape[1], tn), lambda s: (layer, 0, jnp.minimum(s, no - 1))),
                  pl.BlockSpec((1, d, tf), lambda s: (layer, 0, jnp.maximum(s - no, 0))),
                  pl.BlockSpec((1, tf, d), lambda s: (layer, jnp.maximum(s - no, 0), 0))],
        out_specs=pl.BlockSpec((rows, d), lambda s: (0, 0)),
        out_shape=jax.ShapeDtypeStruct((rows, d), BF16),
        scratch_shapes=[pltpu.VMEM((rows, d), BF16), pltpu.VMEM((rows, d), BF16), pltpu.VMEM((rows, d), F32)],
        compiler_params=pltpu.CompilerParams(vmem_limit_bytes=60 * 2**20),
        cost_estimate=pl.CostEstimate(flops=2 * rows * d * (d + 2 * f), bytes_accessed=2 * d * (d + 2 * f), transcendentals=0),
        name="mlp",
    )(o, x, g, wo, wu, wd)


def mlp_only_kernel(nf, tm, h_ref, g_ref, wu, wd, y_ref, r_ref, acc_ref):
    s = pl.program_id(0)
    rows, d = h_ref.shape

    @pl.when(s == 0)
    def _():
        def nb(r):
            h = h_ref[pl.ds(r, 128), :]
            r_ref[pl.ds(r, 128), :] = norm_rows(h, g_ref[0])
            acc_ref[pl.ds(r, 128), :] = h.astype(F32)
        row_loop(rows, 128, nb)

    def mb(r):
        z = jnp.dot(r_ref[pl.ds(r, tm), :], wu[0], preferred_element_type=F32)
        z = gelu(z).astype(BF16)
        acc_ref[pl.ds(r, tm), :] += jnp.dot(z, wd[0], preferred_element_type=F32)
    row_loop(rows, tm, mb)

    @pl.when(s == nf - 1)
    def _():
        def nb(r):
            y_ref[pl.ds(r, 128), :] = acc_ref[pl.ds(r, 128), :].astype(BF16)
        row_loop(rows, 128, nb)


def mlp_only_call(h, g, wu, wd, layer, tf=512, tm=512):
    rows, d = h.shape
    f = wu.shape[2]
    nf = f // tf
    return pl.pallas_call(
        functools.partial(mlp_only_kernel, nf, tm),
        grid=(nf,),
        in_specs=[pl.BlockSpec((rows, d), lambda s: (0, 0)), pl.BlockSpec((1, 1, d), lambda s: (layer, 0, 0)),
                  pl.BlockSpec((1, d, tf), lambda s: (layer, 0, s)),
                  pl.BlockSpec((1, tf, d), lambda s: (layer, s, 0))],
        out_specs=pl.BlockSpec((rows, d), lambda s: (0, 0)),
        out_shape=jax.ShapeDtypeStruct((rows, d), BF16),
        scratch_shapes=[pltpu.VMEM((rows, d), BF16), pltpu.VMEM((rows, d), F32)],
        compiler_params=pltpu.CompilerParams(vmem_limit_bytes=48 * 2**20),
        cost_estimate=pl.CostEstimate(flops=4 * rows * d * f, bytes_accessed=4 * d * f, transcendentals=0),
        name="mlp_only",
    )(h, g, wu, wd)


def out_kernel(o_ref, x_ref, wo, h_ref):
    u = jnp.dot(o_ref[...], wo[0], preferred_element_type=F32)
    h_ref[...] = (x_ref[...].astype(F32) + u).astype(BF16)


def out_call(o, x, wo, layer, tn=512):
    rows, d = x.shape
    return pl.pallas_call(
        out_kernel,
        grid=(d // tn,),
        in_specs=[pl.BlockSpec(o.shape, lambda s: (0, 0)), pl.BlockSpec((rows, tn), lambda s: (0, s)),
                  pl.BlockSpec((1, wo.shape[1], tn), lambda s: (layer, 0, s))],
        out_specs=pl.BlockSpec((rows, tn), lambda s: (0, s)),
        out_shape=jax.ShapeDtypeStruct((rows, d), BF16),
        cost_estimate=pl.CostEstimate(flops=2 * rows * d * wo.shape[1], bytes_accessed=2 * d * d, transcendentals=0),
        name="out",
    )(o, x, wo)


def relayout_kernel(wq, wk, wv, oq, ok, ov):
    _, tk, nh, dh = wq.shape
    for w, o in ((wq, oq), (wk, ok), (wv, ov)):
        o[0] = w[0].reshape(tk, nh * dh)


def relayout_call(wq, wk, wv, tk=128):
    nl, d, nh, dh = wq.shape
    ispec = pl.BlockSpec((1, tk, nh, dh), lambda l, s: (l, s, 0, 0))
    ospec = pl.BlockSpec((1, tk, nh * dh), lambda l, s: (l, s, 0))
    out = jax.ShapeDtypeStruct((nl, d, nh * dh), BF16)
    return pl.pallas_call(
        relayout_kernel,
        grid=(nl, d // tk),
        in_specs=[ispec] * 3,
        out_specs=[ospec] * 3,
        out_shape=[out] * 3,
        cost_estimate=pl.CostEstimate(flops=6 * 10**10, bytes_accessed=12 * nl * d * nh * dh, transcendentals=0),
        name="relayout",
    )(wq, wk, wv)


ROPE_BASE = 10000.0


def rope_tables(positions, head_dim):
    inv_freq = ROPE_BASE ** (-jnp.arange(head_dim // 2, dtype=F32) * (2.0 / head_dim))
    angles = positions.astype(F32)[:, None] * inv_freq
    c, s = jnp.cos(angles), jnp.sin(angles)
    return jnp.concatenate([c, c], axis=1), jnp.concatenate([-s, s], axis=1)


def solution(mesh):
    tok_spec = P(None, ("data", "seq"), None)
    in_specs = (tok_spec, P(("data", "seq"))) + (P(),) * 8
    n_dev = mesh.shape["seq"]

    def device_fn(x_loc, pos_loc, w_query, w_key, w_value, w_out, w_up, w_down, g_attn, g_mlp):
        n_seq, shard, d = x_loc.shape
        n_layers, _, n_heads, dh = w_query.shape
        hd = n_heads * dh
        a2a = lambda a: lax.all_to_all(a, "seq", 0, 0, tiled=True)
        pos = lax.all_gather(pos_loc, "seq", tiled=True)
        pos, x_loc = lax.optimization_barrier((pos, x_loc))
        x = a2a(x_loc).reshape(n_dev * shard, d)
        cos, sin = rope_tables(pos, dh)
        wq, wk, wv = relayout_call(w_query, w_key, w_value)
        wo = w_out.reshape(n_layers, hd, d)
        ga, gm = g_attn[:, None, :], g_mlp[:, None, :]
        half = shard // 2
        for l in range(n_layers):
            q, k, v = qkv_call(x, ga, cos, sin, wq, wk, wv, l, tm=1024)
            o = attn_call(q, k, v, dh, hb=4)
            if l < n_layers - 1:
                x = mlp_call(o, x, gm, wo, w_up, w_down, l, tf=1024, tm=1024)
        l = n_layers - 1
        part = lambda a, i: a.reshape(n_dev, shard, a.shape[1])[:, i * half:(i + 1) * half].reshape(n_dev * half, a.shape[1])
        h_a = out_call(part(o, 0), part(x, 0), wo, l)
        h_a = a2a(h_a.reshape(n_dev, half, d))
        y_b = mlp_call(part(o, 1), part(x, 1), gm, wo, w_up, w_down, l, tf=1024, tm=512)
        y_b = a2a(y_b.reshape(n_dev, half, d))
        y_a = mlp_only_call(h_a.reshape(n_dev * half, d), gm, w_up, w_down, l, tf=1024, tm=512).reshape(n_dev, half, d)
        return jnp.concatenate([y_a, y_b], axis=1)

    return jax.shard_map(device_fn, mesh=mesh, in_specs=in_specs, out_specs=tok_spec, check_vma=False)
```

time: 1930 us -> 632 us (0.33)
  waiting for transfers between devices: 732 us -> 22.9 us
  matrix products: 566 us -> 0 us
  Pallas kernels: 0 us -> 538 us
  blocking collectives: 210 us -> 16.1 us
  local copies, waits for them, and re-layouts: 166 us -> 12.1 us
  other arithmetic: 147 us -> 8.13 us
  starting transfers between devices: 89.3 us -> 22.9 us
    all_to_all x10 -> x3, waiting for transfers between devices: 732 us -> 22.9 us  [device_fn(): a2a = lambda a: lax.all_to_all(a, 'seq', 0, 0, tiled=True)]
    dot_general x42 -> x0, matrix products: 566 us -> none  [the longest x3 139 us: layer_step(): jnp.einsum('bsd,df->bsf', normed_mlp, w_up, preferred_element_type=jnp.fl...]
    pallas_call x0 -> x12, Pallas kernels: none -> 538 us  [the longest x3 241 us: mlp_call(): pl.pallas_call(functools.partial(mlp_kernel, no, nf, tm), grid=(no + nf,)...]
    all_to_all x2 -> x0, blocking collectives: 210 us -> none  [layer_step(): attn_loc = lax.all_to_all(attn_heads, 'seq', 1, 2, tiled=True)]
    all_to_all x10 -> x3, starting transfers between devices: 89.3 us -> 22.9 us  [device_fn(): a2a = lambda a: lax.all_to_all(a, 'seq', 0, 0, tiled=True)]
    another operation x3 -> x0, other arithmetic: 58.3 us -> none
    reduce_sum x13 -> x0, other arithmetic: 58.1 us -> none  [the longest x12 54.1 us: one_block(): row_sum = jnp.sum(exp_f32, axis=-1)]
    all_to_all x12 -> x0, local copies, waits for them, and re-layouts: 55.7 us -> none  [the longest x3 16.8 us: layer_step(): q_all = lax.all_to_all(q_loc, 'seq', 2, 1, tiled=True)]
  transfers between devices with their start and end apart: 10 -> 3, of which waited for: 10 -> 2; matrix products, arithmetic and copies ran while one was open for 10% -> 1% of each run, Pallas kernels for 0% -> 27%
where the time goes in v1:
time: 632 us; the launch traced here: 621 us
  Pallas kernels  538 us (85%)
  starting transfers between devices  22.9 us (4%)
  waiting for transfers between devices  22.9 us (4%)
  blocking collectives  16.1 us (3%)
  local copies, waits for them, and re-layouts  12.1 us (2%)
  other arithmetic  8.13 us (1%)
    pallas_call x3, Pallas kernels, mlp_call(): pl.pallas_call(functools.partial(mlp_kernel, no, nf, tm), grid=(no + nf,)...  241 us
    pallas_call x3, Pallas kernels, qkv_call(): pl.pallas_call(functools.partial(qkv_kernel, nq, tm), grid=(3 * nq,), in_...  120 us
    pallas_call x1, Pallas kernels, relayout_call(): pl.pallas_call(relayout_kernel, grid=(nl, d // tk), in_specs=[ispec] * 3,...  69.7 us
    pallas_call x3, Pallas kernels, attn_call(): pl.pallas_call(functools.partial(attn_kernel, dh, tq), grid=(hd // dh //...  53.9 us
    pallas_call x1, Pallas kernels, mlp_only_call(): pl.pallas_call(functools.partial(mlp_only_kernel, nf, tm), grid=(nf,), in...  43.6 us
    all_to_all x3, starting transfers between devices, device_fn(): a2a = lambda a: lax.all_to_all(a, 'seq', 0, 0, tiled=True)  22.9 us
    all_to_all x3, waiting for transfers between devices, device_fn(): a2a = lambda a: lax.all_to_all(a, 'seq', 0, 0, tiled=True)  22.9 us
    optimization_barrier x1, blocking collectives, device_fn(): pos, x_loc = lax.optimization_barrier((pos, x_loc))  16.1 us
  transfers between devices with their start and end apart: 3, of which 2 were waited for; matrix products, arithmetic and copies ran while one was open for 1% of the time, Pallas kernels for 27%

profile of v1, /device:TPU:21, one launch (start us, length us, event | category | flops | bytes accessed | tf_op | source)
XLA Modules:
  0.0 620.9 jit_solution(15292353289385284776)
XLA Ops:
  2.8 16.1 %all-reduce = s32[1024]{0:T(1024)S(1)} all-reduce(s32[1024]{0:T(1024)S(1)} %dynamic-update-slice), channel_id=1, replica_groups=mesh['data'=4,'seq'=16] {'seq'}, use_global_device_ids=true, to_apply=%add | all-reduce | flops 1024 | bytes 8192 | tf_op jit(solution)/shard_map/optimization_barrier | solution.py:293
  18.9 7.5 %all-to-all-start = ((bf16[16,64,2048]{2,1,0:T(8,128)(2,1)}), bf16[16,64,2048]{2,1,0:T(8,128)(2,1)}, u32[]{:S(2)}, u32[]{:S(2)}) async-start(bf16[16,64,2048]{2,1,0:T(8,128)(2,1)} %param.10), calls=%async_computation | async-start | bytes 8388608 | tf_op jit(solution)/shard_map/all_to_all | solution.py:291
  27.6 1.9 fusion
  29.5 1.4 pad_maximum_fusion.1
  30.9 69.7 %relayout.1 = (bf16[3,2048,2048]{2,1,0:T(8,128)(2,1)}, bf16[3,2048,2048]{2,1,0:T(8,128)(2,1)}, bf16[3,2048,2048]{2,1,0:T(8,128)(2,1)}) custom-call(bf16[3,2048,16,128]{3,2,1,0:T(8,128)(2,1)} %wq.1, bf16[3,2048,16,128]{3,2,1,0:T(8,128)(2,1)} %wk.1, bf16[3,2048,16,128]{3,2,1,0:T(8,128)(2,1)} %wv.1), custom_call_target="tpu_custom_call" | custom-call | flops 60000002048 | bytes 150994944 | tf_op jit(solution)/shard_map/relayout/pallas_call | solution.py:261
  100.6 19.0 %all-to-all-done = bf16[16,64,2048]{2,1,0:T(8,128)(2,1)} async-done(((bf16[16,64,2048]{2,1,0:T(8,128)(2,1)}), bf16[16,64,2048]{2,1,0:T(8,128)(2,1)}, u32[]{:S(2)}, u32[]{:S(2)}) %all-to-all-start) | async-done | bytes 4194336 | tf_op jit(solution)/shard_map/all_to_all | solution.py:291
  119.6 39.6 %qkv.3 = (bf16[1024,2048]{1,0:T(8,128)(2,1)}, bf16[1024,2048]{1,0:T(8,128)(2,1)}, bf16[1024,2048]{1,0:T(8,128)(2,1)}) custom-call(bf16[1024,2048]{1,0:T(8,128)(2,1)} %bitcast.1.x_ref, f32[3,1,2048]{2,1,0:T(1,128)} %broadcast_in_dim.8.g_ref, f32[1024,128]{1,0:T(8,128)} %get-tuple-element.40.cos_ref, f32[1024,128]{1,0:T(8,128)} %get-tuple-element.41.sin_ref, ...), custom_call_target="tpu_custom_call" | custom-call | flops 25769803776 | bytes 25165824 | tf_op jit(solution)/shard_map/qkv/pallas_call | solution.py:73
  159.2 18.0 %attn.3.o_ref = bf16[1024,2048]{1,0:T(8,128)(2,1)} custom-call(bf16[1024,2048]{1,0:T(8,128)(2,1)} %get-tuple-element.24.q_ref, bf16[1024,2048]{1,0:T(8,128)(2,1)} %get-tuple-element.25.k_ref, bf16[1024,2048]{1,0:T(8,128)(2,1)} %get-tuple-element.26.v_ref), custom_call_target="tpu_custom_call" | custom-call | flops 4294967296 | bytes 16777216 | tf_op jit(solution)/shard_map/attn/pallas_call | solution.py:118
  177.2 94.3 %mlp.3.x_ref = bf16[1024,2048]{1,0:T(8,128)(2,1)} custom-call(bf16[1024,2048]{1,0:T(8,128)(2,1)} %attn.3.o_ref, bf16[1024,2048]{1,0:T(8,128)(2,1)} %bitcast.1.x_ref, f32[3,1,2048]{2,1,0:T(1,128)} %broadcast_in_dim.9.g_ref, bf16[3,2048,2048]{2,1,0:T(8,128)(2,1)} %bitcast.15, bf16[3,2048,8192]{2,1,0:T(8,128)(2,1)} %wu.7, bf16[3,8192,2048]{2,1,0:T(8,128)(2,1)} %wd.7), custom_call_target="tpu_custom_call" | custom-call | flops 77309411328 | bytes 75497472 | tf_op jit(solution)/shard_map/mlp/pallas_call | solution.py:171
  271.5 40.1 %qkv.4 = (bf16[1024,2048]{1,0:T(8,128)(2,1)}, bf16[1024,2048]{1,0:T(8,128)(2,1)}, bf16[1024,2048]{1,0:T(8,128)(2,1)}) custom-call(bf16[1024,2048]{1,0:T(8,128)(2,1)} %mlp.3.x_ref, f32[3,1,2048]{2,1,0:T(1,128)} %broadcast_in_dim.8.g_ref, f32[1024,128]{1,0:T(8,128)} %get-tuple-element.40.cos_ref, f32[1024,128]{1,0:T(8,128)} %get-tuple-element.41.sin_ref, ...), custom_call_target="tpu_custom_call" | custom-call | flops 25769803776 | bytes 25165824 | tf_op jit(solution)/shard_map/qkv/pallas_call | solution.py:73
  311.6 18.0 %attn.4.o_ref = bf16[1024,2048]{1,0:T(8,128)(2,1)} custom-call(bf16[1024,2048]{1,0:T(8,128)(2,1)} %get-tuple-element.27.q_ref, bf16[1024,2048]{1,0:T(8,128)(2,1)} %get-tuple-element.28.k_ref, bf16[1024,2048]{1,0:T(8,128)(2,1)} %get-tuple-element.29.v_ref), custom_call_target="tpu_custom_call" | custom-call | flops 4294967296 | bytes 16777216 | tf_op jit(solution)/shard_map/attn/pallas_call | solution.py:118
  329.6 94.3 %mlp.4.x_ref = bf16[1024,2048]{1,0:T(8,128)(2,1)} custom-call(bf16[1024,2048]{1,0:T(8,128)(2,1)} %attn.4.o_ref, bf16[1024,2048]{1,0:T(8,128)(2,1)} %mlp.3.x_ref, f32[3,1,2048]{2,1,0:T(1,128)} %broadcast_in_dim.9.g_ref, bf16[3,2048,2048]{2,1,0:T(8,128)(2,1)} %bitcast.16, bf16[3,2048,8192]{2,1,0:T(8,128)(2,1)} %wu.7, bf16[3,8192,2048]{2,1,0:T(8,128)(2,1)} %wd.7), custom_call_target="tpu_custom_call" | custom-call | flops 77309411328 | bytes 75497472 | tf_op jit(solution)/shard_map/mlp/pallas_call | solution.py:171
  423.9 40.4 %qkv.5 = (bf16[1024,2048]{1,0:T(8,128)(2,1)}, bf16[1024,2048]{1,0:T(8,128)(2,1)}, bf16[1024,2048]{1,0:T(8,128)(2,1)}) custom-call(bf16[1024,2048]{1,0:T(8,128)(2,1)} %mlp.4.x_ref, f32[3,1,2048]{2,1,0:T(1,128)} %broadcast_in_dim.8.g_ref, f32[1024,128]{1,0:T(8,128)} %get-tuple-element.40.cos_ref, f32[1024,128]{1,0:T(8,128)} %get-tuple-element.41.sin_ref, ...), custom_call_target="tpu_custom_call" | custom-call | flops 25769803776 | bytes 25165824 | tf_op jit(solution)/shard_map/qkv/pallas_call | solution.py:73
  464.3 2.6 fusion.1
  466.8 18.0 %attn.5 = bf16[1024,2048]{1,0:T(8,128)(2,1)} custom-call(bf16[1024,2048]{1,0:T(8,128)(2,1)} %get-tuple-element.30.q_ref, bf16[1024,2048]{1,0:T(8,128)(2,1)} %get-tuple-element.31.k_ref, bf16[1024,2048]{1,0:T(8,128)(2,1)} %get-tuple-element.32.v_ref), custom_call_target="tpu_custom_call" | custom-call | flops 4294967296 | bytes 16777216 | tf_op jit(solution)/shard_map/attn/pallas_call | solution.py:118
  484.8 4.9 fusion.2
  489.7 9.1 %out.1 = bf16[512,2048]{1,0:T(8,128)(2,1)} custom-call(bf16[512,2048]{1,0:T(8,128)(2,1)} %bitcast.25, bf16[512,2048]{1,0:T(8,128)(2,1)} %bitcast.24, bf16[3,2048,2048]{2,1,0:T(8,128)(2,1)} %bitcast.17), custom_call_target="tpu_custom_call" | custom-call | flops 4294967296 | bytes 8388608 | tf_op jit(solution)/shard_map/out/pallas_call | solution.py:238
  498.8 8.2 %all-to-all-start.1 = ((bf16[16,32,2048]{2,1,0:T(8,128)(2,1)}), bf16[16,32,2048]{2,1,0:T(8,128)(2,1)S(1)}, u32[]{:S(2)}, u32[]{:S(2)}) async-start(bf16[16,32,2048]{2,1,0:T(8,128)(2,1)} %bitcast.23), calls=%async_computation.1 | async-start | bytes 4194304 | tf_op jit(solution)/shard_map/all_to_all | solution.py:291
  507.1 52.5 %mlp.5 = bf16[512,2048]{1,0:T(8,128)(2,1)} custom-call(bf16[512,2048]{1,0:T(8,128)(2,1)} %bitcast.22, bf16[512,2048]{1,0:T(8,128)(2,1)} %bitcast.21, f32[3,1,2048]{2,1,0:T(1,128)} %broadcast_in_dim.9.g_ref, bf16[3,2048,2048]{2,1,0:T(8,128)(2,1)} %bitcast.18, bf16[3,2048,8192]{2,1,0:T(8,128)(2,1)} %wu.7, bf16[3,8192,2048]{2,1,0:T(8,128)(2,1)} %wd.7), custom_call_target="tpu_custom_call" | custom-call | flops 38654705664 | bytes 75497472 | tf_op jit(solution)/shard_map/mlp/pallas_call | solution.py:171
  559.6 7.3 %all-to-all-start.2 = ((bf16[16,32,2048]{2,1,0:T(8,128)(2,1)}), bf16[16,32,2048]{2,1,0:T(8,128)(2,1)}, u32[]{:S(2)}, u32[]{:S(2)}) async-start(bf16[16,32,2048]{2,1,0:T(8,128)(2,1)} %bitcast.20), calls=%async_computation.2 | async-start | bytes 4194304 | tf_op jit(solution)/shard_map/all_to_all | solution.py:291
  566.9 43.6 %mlp_only.1 = bf16[512,2048]{1,0:T(8,128)(2,1)S(1)} custom-call(bf16[512,2048]{1,0:T(8,128)(2,1)S(1)} %bitcast.13, f32[3,1,2048]{2,1,0:T(1,128)S(1)} %copy-done.1, bf16[3,2048,8192]{2,1,0:T(8,128)(2,1)} %wu.7, bf16[3,8192,2048]{2,1,0:T(8,128)(2,1)} %wd.7), custom_call_target="tpu_custom_call" | custom-call | flops 34359738368 | bytes 67108864 | tf_op jit(solution)/shard_map/mlp_only/pallas_call | solution.py:216
  610.4 1.3 copy-done
  611.7 3.9 all-to-all-done.2
  615.6 4.8 pad_maximum_fusion
  (17 shorter events, 3.4 us)
Async XLA Ops:
  18.9 7.5 %copy-start.3 = (f32[3,2048]{1,0:T(4,128)S(1)}, f32[3,2048]{1,0:T(4,128)}, u32[]{:S(2)}) copy-start(f32[3,2048]{1,0:T(4,128)} %param.19) | copy-start | bytes 73732
  18.9 8.1 %copy-start.4 = (f32[3,2048]{1,0:T(4,128)S(1)}, f32[3,2048]{1,0:T(4,128)}, u32[]{:S(2)}) copy-start(f32[3,2048]{1,0:T(4,128)} %param.18) | copy-start | bytes 73732
  18.9 100.7 %all-to-all-start = ((bf16[16,64,2048]{2,1,0:T(8,128)(2,1)}), bf16[16,64,2048]{2,1,0:T(8,128)(2,1)}, u32[]{:S(2)}, u32[]{:S(2)}) async-start(bf16[16,64,2048]{2,1,0:T(8,128)(2,1)} %param.10), calls=%async_computation | async-start | bytes 8388608 | tf_op jit(solution)/shard_map/all_to_all | solution.py:291
  423.9 40.4 %copy-start.2 = (bf16[1024,2048]{1,0:T(8,128)(2,1)S(1)}, bf16[1024,2048]{1,0:T(8,128)(2,1)}, u32[]{:S(2)}) copy-start(bf16[1024,2048]{1,0:T(8,128)(2,1)} %mlp.4.x_ref) | copy-start | bytes 12582916
  498.8 60.8 %all-to-all-start.1 = ((bf16[16,32,2048]{2,1,0:T(8,128)(2,1)}), bf16[16,32,2048]{2,1,0:T(8,128)(2,1)S(1)}, u32[]{:S(2)}, u32[]{:S(2)}) async-start(bf16[16,32,2048]{2,1,0:T(8,128)(2,1)} %bitcast.23), calls=%async_computation.1 | async-start | bytes 4194304 | tf_op jit(solution)/shard_map/all_to_all | solution.py:291
  559.6 7.3 %copy-start.1 = (f32[3,1,2048]{2,1,0:T(1,128)S(1)}, f32[3,1,2048]{2,1,0:T(1,128)}, u32[]{:S(2)}) copy-start(f32[3,1,2048]{2,1,0:T(1,128)} %broadcast_in_dim.9.g_ref) | copy-start | bytes 73732
  559.6 56.1 %all-to-all-start.2 = ((bf16[16,32,2048]{2,1,0:T(8,128)(2,1)}), bf16[16,32,2048]{2,1,0:T(8,128)(2,1)}, u32[]{:S(2)}, u32[]{:S(2)}) async-start(bf16[16,32,2048]{2,1,0:T(8,128)(2,1)} %bitcast.20), calls=%async_computation.2 | async-start | bytes 4194304 | tf_op jit(solution)/shard_map/all_to_all | solution.py:291
  610.4 1.3 copy-start

commit v2 on v1

v2 whole, which is shorter than its diff:
```python
import functools
import jax
import jax.numpy as jnp
from jax import lax
from jax.experimental import pallas as pl
from jax.experimental.pallas import tpu as pltpu
from jax.sharding import PartitionSpec as P

EPS = 1e-6
F32 = jnp.float32
BF16 = jnp.bfloat16


def norm_rows(x, g):
    x = x.astype(F32)
    return (x * lax.rsqrt(jnp.mean(x * x, axis=-1, keepdims=True) + EPS) * g).astype(BF16)


def gelu(x):
    h = 0.5 * x
    return h * jnp.tanh(x * (0.7978845608028654 + 0.035677408136300125 * (x * x))) + h


def row_loop(rows, tile, body):
    if rows == tile:
        body(0)
        return
    def step(i, c):
        body(pl.multiple_of(i * tile, tile))
        return c
    lax.fori_loop(0, rows // tile, step, 0)


def attention(dh, tq, q_ref, k_ref, v_ref, o_ref):
    rows, width = q_ref.shape
    scale = dh ** -0.5 * 1.4426950408889634
    keep = lax.broadcasted_iota(jnp.int32, (tq, tq), 1) <= lax.broadcasted_iota(jnp.int32, (tq, tq), 0)
    jobs = [(slice(h * dh, (h + 1) * dh), i) for h in range(width // dh) for i in range(rows // tq)]

    def score(cs, i):
        n = (i + 1) * tq
        return lax.dot_general(q_ref[i * tq:n, cs], k_ref[:n, cs], (((1,), (1,)), ((), ())), preferred_element_type=F32)

    nxt = score(*jobs[0])
    for j, (cs, i) in enumerate(jobs):
        s = nxt
        if j + 1 < len(jobs):
            nxt = score(*jobs[j + 1])
        n = (i + 1) * tq
        sd = jnp.where(keep, s[:, n - tq:], -1e30)
        s = jnp.concatenate([s[:, :n - tq], sd], axis=1) if i else sd
        m = jnp.max(s, axis=1, keepdims=True)
        e = jnp.exp2((s - m) * scale)
        l = jnp.sum(e, axis=1, keepdims=True)
        o = jnp.dot(e.astype(BF16), v_ref[:n, cs], preferred_element_type=F32)
        o_ref[i * tq:n, cs] = (o / l).astype(BF16)


def layers_kernel(cfg, x_ref, ga_ref, gm_ref, tab_ref, wqkv, wo, wu, wd, ha_ref, hb_ref, n_ref, qkv_ref, acc_ref):
    nx, nq, na, no, nf, last, tq, to, tm = cfg
    t = pl.program_id(0) - nx
    per = nq + na + no + nf
    layer = jnp.maximum(t, 0) // per
    p = lax.rem(jnp.maximum(t, 0), per)
    dh = tab_ref.shape[2]
    ng, rows, gw = qkv_ref.shape
    d = acc_ref.shape[1]

    @pl.when(t < 0)
    def _():
        xr = x_ref.shape[0]
        base = (t + nx) * xr
        def nb(r):
            x = x_ref[pl.ds(r, 128), :]
            rs = pl.ds(pl.multiple_of(base + r, 128), 128)
            n_ref[rs, :] = norm_rows(x, ga_ref[0])
            acc_ref[rs, :] = x.astype(F32)
        row_loop(xr, 128, nb)

    @pl.when((t >= 0) & (p < nq))
    def _():
        tn = wqkv.shape[2]
        k = tn // gw
        tab = jnp.where(p * k < 2 * ng // 3, 0, 1)
        for r in range(0, rows, tq):
            u = jnp.dot(n_ref[r:r + tq, :], wqkv[0], preferred_element_type=F32)
            cs = tab_ref[tab, r:r + tq, :]
            sc = pltpu.roll(cs, dh // 2, 1)
            lo = lax.broadcasted_iota(jnp.int32, cs.shape, 1) < dh // 2
            c = jnp.where(lo, cs, sc)
            sn = jnp.where(lo, -sc, cs)
            for h in range(tn // dh):
                uh = u[:, h * dh:(h + 1) * dh]
                g, o = divmod(h * dh, gw)
                qkv_ref[p * k + g, r:r + tq, o:o + dh] = (uh * c + pltpu.roll(uh, dh // 2, 1) * sn).astype(BF16)

    @pl.when((p >= nq) & (p < nq + na))
    def _():
        a = p - nq
        attention(dh, 256, qkv_ref.at[a], qkv_ref.at[na + a], qkv_ref.at[2 * na + a], qkv_ref.at[a])

    @pl.when((p >= nq + na) & (p < nq + na + no))
    def _():
        tn = wo.shape[2]
        half = ha_ref.shape[1]
        nd = to // (2 * half)
        cs = pl.ds(pl.multiple_of((p - nq - na) * tn, tn), tn)
        for r in range(0, rows, to):
            o = jnp.concatenate([qkv_ref[a, r:r + to, :] for a in range(na)], axis=1)
            u = jnp.dot(o, wo[0], preferred_element_type=F32)
            h = (acc_ref[r:r + to, cs] + u).astype(BF16)
            acc_ref[r:r + to, cs] = h.astype(F32)
            h = h.reshape(nd, 2 * half, tn)
            i = r // (2 * half)
            ha_ref[i:i + nd] = h[:, :half]
            hb_ref[i:i + nd] = h[:, half:]

    @pl.when(p == nq + na + no)
    def _():
        def nb(r):
            n_ref[pl.ds(r, 128), :] = norm_rows(acc_ref[pl.ds(r, 128), :], gm_ref[0])
        row_loop(rows, 128, nb)

    @pl.when(p >= nq + na + no)
    def _():
        for r in range(0, rows, tm):
            z = jnp.dot(n_ref[r:r + tm, :], wu[0], preferred_element_type=F32)
            z = gelu(z).astype(BF16)
            acc_ref[r:r + tm, :] += jnp.dot(z, wd[0], preferred_element_type=F32)

    @pl.when(p == per - 1)
    def _():
        def nb(r):
            y = acc_ref[pl.ds(r, 128), :].astype(BF16)
            acc_ref[pl.ds(r, 128), :] = y.astype(F32)
            n_ref[pl.ds(r, 128), :] = norm_rows(y, ga_ref[0])
        row_loop(rows, 128, nb)


def layers_call(x, ga, gm, table, wqkv, wo, wu, wd, n_dev, tnq=1024, tno=512, tf=1024, gw=512, xr=128, tq=256, to=256, tm=1024):
    rows, d = x.shape
    nl, _, hd3 = wqkv.shape
    hd = hd3 // 3
    f = wu.shape[2]
    half = rows // n_dev // 2
    nx, nq, na, no, nf, last = rows // xr, hd3 // tnq, hd // gw, d // tno, f // tf, nl - 1
    per = nq + na + no + nf
    grid = nx + last * per + nq + na + no

    def lp(s):
        t = jnp.maximum(s - nx, 0)
        return t // per, lax.rem(t, per)

    def gain_map(s):
        l, p = lp(s)
        return jnp.minimum(l + jnp.where(p == per - 1, 1, 0), last), 0, 0

    def qkv_map(s):
        l, p = lp(s)
        return l, 0, jnp.minimum(p, nq - 1)

    def out_map(s):
        l, p = lp(s)
        return l, 0, jnp.clip(p - nq - na, 0, no - 1)

    def ff_map(s):
        l, p = lp(s)
        return jnp.minimum(l, last - 1), jnp.where(l == last, nf - 1, jnp.clip(p - nq - na - no, 0, nf - 1))

    def up_map(s):
        l, c = ff_map(s)
        return l, 0, c

    def down_map(s):
        l, c = ff_map(s)
        return l, c, 0

    def h_map(s):
        l, p = lp(s)
        return 0, 0, jnp.where(l == last, jnp.clip(p - nq - na, 0, no - 1), 0)

    once = pl.Buffered(1)
    tab = pl.BlockSpec(table.shape, lambda s: (0, 0, 0), pipeline_mode=once)
    out = jax.ShapeDtypeStruct((n_dev, half, d), BF16)
    return pl.pallas_call(
        functools.partial(layers_kernel, (nx, nq, na, no, nf, last, tq, to, tm)),
        grid=(grid,),
        in_specs=[pl.BlockSpec((xr, d), lambda s: (jnp.minimum(s, nx - 1), 0)),
                  pl.BlockSpec((1, 1, d), gain_map), pl.BlockSpec((1, 1, d), lambda s: (lp(s)[0], 0, 0)), tab,
                  pl.BlockSpec((1, d, tnq), qkv_map), pl.BlockSpec((1, hd, tno), out_map),
                  pl.BlockSpec((1, d, tf), up_map), pl.BlockSpec((1, tf, d), down_map)],
        out_specs=[pl.BlockSpec((n_dev, half, tno), h_map)] * 2,
        out_shape=[out, out],
        scratch_shapes=[pltpu.VMEM((rows, d), BF16), pltpu.VMEM((3 * na, rows, gw), BF16), pltpu.VMEM((rows, d), F32)],
        compiler_params=pltpu.CompilerParams(vmem_limit_bytes=67043328),
        cost_estimate=pl.CostEstimate(flops=2 * rows * (nl * d * 4 * hd + 2 * last * d * f), bytes_accessed=2 * (nl * d * 4 * hd + 2 * last * d * f), transcendentals=0),
        name="layers",
    )(x, ga, gm, table, wqkv, wo, wu, wd)


def mlp_only_kernel(nf, tm, h_ref, g_ref, wu, wd, y_ref, r_ref, acc_ref):
    s = pl.program_id(0)
    rows, d = h_ref.shape

    @pl.when(s == 0)
    def _():
        def nb(r):
            h = h_ref[pl.ds(r, 128), :]
            r_ref[pl.ds(r, 128), :] = norm_rows(h, g_ref[0])
            acc_ref[pl.ds(r, 128), :] = h.astype(F32)
        row_loop(rows, 128, nb)

    def mb(r):
        z = jnp.dot(r_ref[pl.ds(r, tm), :], wu[0], preferred_element_type=F32)
        z = gelu(z).astype(BF16)
        acc_ref[pl.ds(r, tm), :] += jnp.dot(z, wd[0], preferred_element_type=F32)
    row_loop(rows, tm, mb)

    @pl.when(s == nf - 1)
    def _():
        def nb(r):
            y_ref[pl.ds(r, 128), :] = acc_ref[pl.ds(r, 128), :].astype(BF16)
        row_loop(rows, 128, nb)


def mlp_only_call(h, g, wu, wd, layer, tf=512, tm=512):
    rows, d = h.shape
    f = wu.shape[2]
    nf = f // tf
    return pl.pallas_call(
        functools.partial(mlp_only_kernel, nf, tm),
        grid=(nf,),
        in_specs=[pl.BlockSpec((rows, d), lambda s: (0, 0)), pl.BlockSpec((1, 1, d), lambda s: (layer, 0, 0)),
                  pl.BlockSpec((1, d, tf), lambda s: (layer, 0, s)),
                  pl.BlockSpec((1, tf, d), lambda s: (layer, s, 0))],
        out_specs=pl.BlockSpec((rows, d), lambda s: (0, 0)),
        out_shape=jax.ShapeDtypeStruct((rows, d), BF16),
        scratch_shapes=[pltpu.VMEM((rows, d), BF16), pltpu.VMEM((rows, d), F32)],
        compiler_params=pltpu.CompilerParams(vmem_limit_bytes=60 * 2**20),
        cost_estimate=pl.CostEstimate(flops=4 * rows * d * f, bytes_accessed=4 * d * f, transcendentals=0),
        name="mlp_only",
    )(h, g, wu, wd)


def relayout_kernel(wq, wk, wv, o_ref):
    _, tk, nh, dh = wq.shape
    hd = nh * dh
    for i, w in enumerate((wq, wk, wv)):
        o_ref[0, :, i * hd:(i + 1) * hd] = w[0].reshape(tk, hd)


def relayout_call(wq, wk, wv, tk=128):
    nl, d, nh, dh = wq.shape
    return pl.pallas_call(
        relayout_kernel,
        grid=(nl, d // tk),
        in_specs=[pl.BlockSpec((1, tk, nh, dh), lambda l, s: (l, s, 0, 0))] * 3,
        out_specs=pl.BlockSpec((1, tk, 3 * nh * dh), lambda l, s: (l, s, 0)),
        out_shape=jax.ShapeDtypeStruct((nl, d, 3 * nh * dh), BF16),
        cost_estimate=pl.CostEstimate(flops=6 * 10**10, bytes_accessed=12 * nl * d * nh * dh, transcendentals=0),
        name="relayout",
    )(wq, wk, wv)


ROPE_BASE = 10000.0


def rope_tables(positions, head_dim):
    inv_freq = ROPE_BASE ** (-jnp.arange(head_dim // 2, dtype=F32) * (2.0 / head_dim))
    angles = positions.astype(F32)[:, None] * inv_freq
    c, s = jnp.cos(angles), jnp.sin(angles)
    one, zero = jnp.ones_like(c), jnp.zeros_like(s)
    return jnp.stack([jnp.concatenate([c, s], axis=1), jnp.concatenate([one, zero], axis=1)])


def solution(mesh):
    tok_spec = P(None, ("data", "seq"), None)
    in_specs = (tok_spec, P(("data", "seq"))) + (P(),) * 8
    n_dev = mesh.shape["seq"]

    def device_fn(x_loc, pos_loc, w_query, w_key, w_value, w_out, w_up, w_down, g_attn, g_mlp):
        n_seq, shard, d = x_loc.shape
        n_layers, _, n_heads, dh = w_query.shape
        hd = n_heads * dh
        a2a = lambda a: lax.all_to_all(a, "seq", 0, 0, tiled=True)
        pos = a2a(jnp.broadcast_to(pos_loc[None], (n_dev, shard))).reshape(n_dev * shard)
        x = a2a(x_loc).reshape(n_dev * shard, d)
        table = rope_tables(pos, dh)
        wqkv = relayout_call(w_query, w_key, w_value)
        wo = w_out.reshape(n_layers, hd, d)
        ga, gm = g_attn[:, None, :], g_mlp[:, None, :]
        half = shard // 2
        last = n_layers - 1

        h_a, h_b = layers_call(x, ga, gm, table, wqkv, wo, w_up, w_down, n_dev)
        mlp = lambda h: mlp_only_call(h.reshape(n_dev * half, d), gm, w_up, w_down, last, tf=1024, tm=512).reshape(n_dev, half, d)
        h_a = a2a(h_a)
        y_b = a2a(mlp(h_b))
        y_a = mlp(h_a)
        return jnp.concatenate([y_a, y_b], axis=1)

    return jax.shard_map(device_fn, mesh=mesh, in_specs=in_specs, out_specs=tok_spec, check_vma=False)
```

time: 632 us -> 599 us (0.948); the launches traced: 621 us -> 597 us
  Pallas kernels: 538 us -> 525 us
  local copies, waits for them, and re-layouts: 12.1 us -> 3.34 us
    pallas_call x11 -> x2, Pallas kernels: 494 us -> 434 us  [the longest x1 364 us: layers_call(): pl.pallas_call(functools.partial(layers_kernel, (nx, nq, na, no, nf, last...]
    pallas_call x1 -> x2, Pallas kernels: 43.6 us -> 91 us  [mlp_only_call(): pl.pallas_call(functools.partial(mlp_only_kernel, nf, tm), grid=(nf,), in...]
    all_to_all x0 -> x1, blocking collectives: none -> 17.6 us  [device_fn(): a2a = lambda a: lax.all_to_all(a, 'seq', 0, 0, tiled=True)]
    optimization_barrier x1 -> x0, blocking collectives: 16.1 us -> none  [device_fn(): pos, x_loc = lax.optimization_barrier((pos, x_loc))]
    slice x2 -> x0, local copies, waits for them, and re-layouts: 7.44 us -> none  [device_fn(): a.reshape(n_dev, shard, a.shape[1])[:, i * half:(i + 1) * half]]
  transfers between devices with their start and end apart: 3 -> 3, of which waited for: 2 -> 3; matrix products, arithmetic and copies ran while one was open for 1% -> 1% of each run, Pallas kernels for 27% -> 27%
where the time goes in v2:
time: 599 us; the launch traced here: 597 us
  Pallas kernels  525 us (88%)
  waiting for transfers between devices  25.4 us (4%)
  starting transfers between devices  18.1 us (3%)
  blocking collectives  17.6 us (3%)
  other arithmetic  7.31 us (1%)
    pallas_call x1, Pallas kernels, layers_call(): pl.pallas_call(functools.partial(layers_kernel, (nx, nq, na, no, nf, last...  364 us
    pallas_call x2, Pallas kernels, mlp_only_call(): pl.pallas_call(functools.partial(mlp_only_kernel, nf, tm), grid=(nf,), in...  91 us
    pallas_call x1, Pallas kernels, relayout_call(): pl.pallas_call(relayout_kernel, grid=(nl, d // tk), in_specs=[pl.BlockSpe...  69.8 us
    all_to_all x3, waiting for transfers between devices, device_fn(): a2a = lambda a: lax.all_to_all(a, 'seq', 0, 0, tiled=True)  25.4 us
    all_to_all x3, starting transfers between devices, device_fn(): a2a = lambda a: lax.all_to_all(a, 'seq', 0, 0, tiled=True)  18.1 us
    all_to_all x1, blocking collectives, device_fn(): a2a = lambda a: lax.all_to_all(a, 'seq', 0, 0, tiled=True)  17.6 us
  transfers between devices with their start and end apart: 3, of which 3 were waited for; matrix products, arithmetic and copies ran while one was open for 1% of the time, Pallas kernels for 27%

profile of v2, /device:TPU:21, one launch (start us, length us, event | category | flops | bytes accessed | tf_op | source)
XLA Modules:
  0.0 597.0 jit_solution(2191085856098130759)
XLA Ops:
  0.0 0.7 broadcast_in_dim.20
  0.7 17.6 %all_to_all.21 = s32[16,1,64]{2,1,0:T(1,128)S(1)} all-to-all(s32[16,1,64]{2,1,0:T(1,128)S(1)} %broadcast_in_dim.20), channel_id=1, replica_groups=mesh['data'=4,'seq'=16] {'seq'}, dimensions={0} | all-to-all | bytes 8192 | tf_op jit(solution)/shard_map/all_to_all | solution.py:285
  18.3 0.0 copy-start.1
  18.3 0.0 copy-start.2
  18.3 5.1 all-to-all-start
  23.3 0.0 copy-done.1
  23.3 0.6 broadcast_in_dim.9.gm_ref.g_ref
  23.9 0.0 copy-done.2
  23.9 0.6 broadcast_in_dim.8.ga_ref
  24.6 69.8 %relayout.1.wqkv = bf16[3,2048,6144]{2,1,0:T(8,128)(2,1)} custom-call(bf16[3,2048,16,128]{3,2,1,0:T(8,128)(2,1)} %wq.1, bf16[3,2048,16,128]{3,2,1,0:T(8,128)(2,1)} %wk.1, bf16[3,2048,16,128]{3,2,1,0:T(8,128)(2,1)} %wv.1), custom_call_target="tpu_custom_call" | custom-call | flops 60000002048 | bytes 150994944 | tf_op jit(solution)/shard_map/relayout/pallas_call | solution.py:254
  94.5 0.1 convert_element_type.11
  94.5 1.9 multiply_cosine_fusion
  96.4 0.2 maximum_bitcast_fusion
  96.7 1.0 pad_maximum_fusion.1.tab_ref
  97.7 18.8 %all-to-all-done = bf16[16,64,2048]{2,1,0:T(8,128)(2,1)} async-done(((bf16[16,64,2048]{2,1,0:T(8,128)(2,1)}), bf16[16,64,2048]{2,1,0:T(8,128)(2,1)}, u32[]{:S(2)}, u32[]{:S(2)}) %all-to-all-start) | async-done | bytes 4194336 | tf_op jit(solution)/shard_map/all_to_all | solution.py:285
  116.6 364.3 %layers.1 = (bf16[16,32,2048]{2,1,0:T(8,128)(2,1)}, bf16[16,32,2048]{2,1,0:T(8,128)(2,1)}) custom-call(bf16[1024,2048]{1,0:T(8,128)(2,1)} %bitcast.x_ref, f32[3,1,2048]{2,1,0:T(1,128)} %broadcast_in_dim.8.ga_ref, f32[3,1,2048]{2,1,0:T(1,128)} %broadcast_in_dim.9.gm_ref.g_ref, f32[2,1024,128]{2,1,0:T(8,128)} %pad_maximum_fusion.1.tab_ref, ...), custom_call_target="tpu_custom_call" | custom-call | flops 240518168576 | bytes 234881024 | tf_op jit(solution)/shard_map/layers/pallas_call | solution.py:185
  480.9 7.6 %all-to-all-start.2 = ((bf16[16,32,2048]{2,1,0:T(8,128)(2,1)}), bf16[16,32,2048]{2,1,0:T(8,128)(2,1)S(1)}, u32[]{:S(2)}, u32[]{:S(2)}) async-start(bf16[16,32,2048]{2,1,0:T(8,128)(2,1)} %get-tuple-element.7), calls=%async_computation.2 | async-start | bytes 4194304 | tf_op jit(solution)/shard_map/all_to_all | solution.py:285
  488.5 45.5 %mlp_only.3 = bf16[512,2048]{1,0:T(8,128)(2,1)} custom-call(bf16[512,2048]{1,0:T(8,128)(2,1)} %bitcast.11, f32[3,1,2048]{2,1,0:T(1,128)} %broadcast_in_dim.9.gm_ref.g_ref, bf16[3,2048,8192]{2,1,0:T(8,128)(2,1)} %wu.5, bf16[3,8192,2048]{2,1,0:T(8,128)(2,1)} %wd.5), custom_call_target="tpu_custom_call" | custom-call | flops 34359738368 | bytes 67108864 | tf_op jit(solution)/shard_map/mlp_only/pallas_call | solution.py:230
  534.1 3.2 all-to-all-done.2
  537.3 1.3 copy-done
  538.6 5.4 all-to-all-start.3
  544.0 45.5 %mlp_only.2 = bf16[512,2048]{1,0:T(8,128)(2,1)} custom-call(bf16[512,2048]{1,0:T(8,128)(2,1)} %bitcast.8, f32[3,1,2048]{2,1,0:T(1,128)} %broadcast_in_dim.9.gm_ref.g_ref, bf16[3,2048,8192]{2,1,0:T(8,128)(2,1)} %wu.5, bf16[3,8192,2048]{2,1,0:T(8,128)(2,1)} %wd.5), custom_call_target="tpu_custom_call" | custom-call | flops 34359738368 | bytes 67108864 | tf_op jit(solution)/shard_map/mlp_only/pallas_call | solution.py:230
  589.5 3.3 all-to-all-done.3
  592.8 4.1 pad_maximum_fusion
  (6 shorter events, 0.1 us)
Async XLA Ops:
  18.3 5.1 copy-start.1
  18.3 5.7 copy-start.2
  18.3 98.3 %all-to-all-start = ((bf16[16,64,2048]{2,1,0:T(8,128)(2,1)}), bf16[16,64,2048]{2,1,0:T(8,128)(2,1)}, u32[]{:S(2)}, u32[]{:S(2)}) async-start(bf16[16,64,2048]{2,1,0:T(8,128)(2,1)} %param.10), calls=%async_computation | async-start | bytes 8388608 | tf_op jit(solution)/shard_map/all_to_all | solution.py:285
  480.9 56.4 %all-to-all-start.2 = ((bf16[16,32,2048]{2,1,0:T(8,128)(2,1)}), bf16[16,32,2048]{2,1,0:T(8,128)(2,1)S(1)}, u32[]{:S(2)}, u32[]{:S(2)}) async-start(bf16[16,32,2048]{2,1,0:T(8,128)(2,1)} %get-tuple-element.7), calls=%async_computation.2 | async-start | bytes 4194304 | tf_op jit(solution)/shard_map/all_to_all | solution.py:285
  537.3 1.3 copy-start
  538.6 54.2 %all-to-all-start.3 = ((bf16[16,32,2048]{2,1,0:T(8,128)(2,1)}), bf16[16,32,2048]{2,1,0:T(8,128)(2,1)S(1)}, u32[]{:S(2)}, u32[]{:S(2)}) async-start(bf16[16,32,2048]{2,1,0:T(8,128)(2,1)} %bitcast.9), calls=%async_computation.3 | async-start | bytes 4194304 | tf_op jit(solution)/shard_map/all_to_all | solution.py:285
